TPU v7x, 32 devices: a whole 2x2x4 slice. The times are simulated.
32 devices in a mesh: gx: 4 (over x, core), gy: 4 (over z), gz: 2 (over y).
Axes of the slice: x: 2, y: 2, z: 4, core: 2. Of those that a mesh axis runs over, the one named last changes fastest.
Arguments:
- outcomes: bfloat16 [24576, 2048], P(('gx', 'gy', 'gz')), may hold values from -6 to 6
- sketch: bfloat16 [24576, 128], P(('gx', 'gy', 'gz')), may hold values from -6 to 6
Outputs:
- left_basis: float32 [24576, 128], P(('gx', 'gy', 'gz'))
- factor: float32 [128, 128], replicated
All inputs are finite; a program needn't handle non-finite values.
Results may differ from a plain program's by a relative error of at most 0.005.
Values may be sent and summed in bfloat16 or wider, within the bound.
A program may use at most 64 MiB of HBM per device.

v0:
```python
import math

import jax
import jax.numpy as jnp
from jax import lax
from jax.sharding import PartitionSpec as P

POWER = 2


def per_device(outcomes, sketch):
    device_count = lax.axis_size(("gx", "gy", "gz"))
    rows_here = outcomes.shape[0]
    day_count = outcomes.shape[1]
    unit_count = rows_here * device_count
    current = sketch
    left_basis = None
    lower_tri = None
    for power_step in range(POWER):
        partial_sum = lax.dot_general(
            outcomes, current, (((0,), (0,)), ((), ())), preferred_element_type=jnp.float32
        )
        summed = lax.psum(partial_sum, ("gx", "gy", "gz"))
        day_weights = (summed / math.sqrt(unit_count)).astype(jnp.bfloat16)
        projected = jnp.dot(outcomes, day_weights, preferred_element_type=jnp.float32)
        projected = projected / math.sqrt(day_count)
        gram_local = jnp.dot(projected.T, projected, precision=lax.Precision.HIGHEST) / unit_count
        gram = lax.psum(gram_local, ("gx", "gy", "gz"))
        lower_tri = jnp.linalg.cholesky(gram)
        left_basis = lax.linalg.triangular_solve(
            lower_tri, projected, left_side=False, lower=True, transpose_a=True
        )
        current = left_basis.astype(jnp.bfloat16)
    return (left_basis, lower_tri.T)


def solution(mesh):
    return jax.shard_map(
        per_device,
        mesh=mesh,
        in_specs=(P(("gx", "gy", "gz"), None), P(("gx", "gy", "gz"), None)),
        out_specs=(P(("gx", "gy", "gz"), None), P()),
        check_vma=False,
    )
```

profile of v0, /device:TPU:1, one launch (start us, length us, event | category | flops | bytes accessed | tf_op | source)
XLA Modules:
  0.0 607.3 jit_solution(11905937048318065328)
XLA Ops:
  7.2 0.0 copy-start
  7.2 0.0 all-reduce.5.cloned.1.call-start
  7.2 1.8 copy-done
  9.1 3.0 fusion.16
  12.0 0.0 all-reduce.5.cloned.1.call-update
  12.1 0.0 all-reduce.7.cloned.1.call-start
  12.1 133.1 %all-reduce.5.cloned.1.call-done = f32[2048,128]{1,0:T(8,128)} async-done(((f32[2048,128]{1,0:T(8,128)}), f32[2048,128]{1,0:T(8,128)}) %all-reduce.5.cloned.1.call-update) | async-done | bytes 1048592 | tf_op jit(solution)/shard_map/psum | solution.py:23
  145.2 2.4 convolution_multiply_fusion.1
  147.6 1.1 convolution_multiply_fusion.3
  148.7 0.0 all-reduce.7.cloned.1.call-update
  148.7 0.0 all-reduce.9.cloned.1.call-start
  148.8 123.7 %all-reduce.7.cloned.1.call-done = f32[128,128]{0,1:T(8,128)} async-done(((f32[128,128]{0,1:T(8,128)}), f32[128,128]{0,1:T(8,128)}) %all-reduce.7.cloned.1.call-update) | async-done | bytes 65552 | tf_op jit(solution)/shard_map/psum | solution.py:28
  272.5 1.6 copy.5
  274.0 1.5 fusion.9
  275.5 13.2 %cholesky.44 = f32[128,128]{1,0:T(8,128)} custom-call(f32[128,128]{1,0:T(8,128)} %fusion.9), custom_call_target="Cholesky" | custom-call | tf_op jit(solution)/shard_map/jit(cholesky)/cholesky | solution.py:29
  288.7 0.9 fusion.12
  289.6 0.6 compare_reduce_fusion.1
  290.2 2.1 fusion.5
  292.4 11.3 %custom-call.6 = f32[1,128,128]{1,2,0:T(8,128)} custom-call(f32[1,128,128]{2,1,0:T(8,128)} %fusion.5), custom_call_target="InvertDiagBlocksLowerTriangular" | custom-call | tf_op jit(solution)/shard_map/triangular_solve/custom-call.0 | solution.py:30
  303.6 1.3 fusion
  305.0 2.4 convolution_bitcast_fusion
  307.4 0.0 all-reduce.9.cloned.1.call-update
  307.4 0.2 all-reduce.11.cloned.1.call-start
  307.6 129.2 %all-reduce.9.cloned.1.call-done = f32[2048,128]{1,0:T(8,128)} async-done(((f32[2048,128]{1,0:T(8,128)}), f32[2048,128]{1,0:T(8,128)}) %all-reduce.9.cloned.1.call-update) | async-done | bytes 1048592 | tf_op jit(solution)/shard_map/psum | solution.py:23
  436.8 2.4 convolution_multiply_fusion
  439.2 1.1 convolution_multiply_fusion.2
  440.3 0.0 all-reduce.11.cloned.1.call-update
  440.4 123.6 %all-reduce.11.cloned.1.call-done = f32[128,128]{0,1:T(8,128)} async-done(((f32[128,128]{0,1:T(8,128)}), f32[128,128]{0,1:T(8,128)}) %all-reduce.11.cloned.1.call-update) | async-done | bytes 65552 | tf_op jit(solution)/shard_map/psum | solution.py:28
  564.0 1.6 copy.7
  565.5 1.5 fusion.7
  567.0 13.2 %cholesky.55 = f32[128,128]{1,0:T(8,128)} custom-call(f32[128,128]{1,0:T(8,128)} %fusion.7), custom_call_target="Cholesky" | custom-call | tf_op jit(solution)/shard_map/jit(cholesky)/cholesky | solution.py:29
  580.2 0.9 select_reduce_fusion
  581.1 0.6 compare_reduce_fusion
  581.7 2.1 fusion.13
  583.9 1.6 copy.9
  585.4 11.3 %custom-call.7 = f32[1,128,128]{1,2,0:T(8,128)} custom-call(f32[1,128,128]{2,1,0:T(8,128)} %get-tuple-element.7), custom_call_target="InvertDiagBlocksLowerTriangular" | custom-call | tf_op jit(solution)/shard_map/triangular_solve/custom-call.0 | solution.py:30
  596.7 2.1 convolution_bitcast_fusion.1
  598.8 1.9 copy.8
Async XLA Ops:
  7.2 1.9 copy-start
  7.2 138.0 %all-reduce.5.cloned.1.call-start = ((), (), s32[]{:S(2)}) async-start(), calls=%async_computation | async-start | bytes 2097152 | tf_op jit(solution)/shard_map/psum | solution.py:23
  12.1 260.4 %all-reduce.7.cloned.1.call-start = ((), (), s32[]{:S(2)}) async-start(), calls=%async_computation.1 | async-start | bytes 131072 | tf_op jit(solution)/shard_map/psum | solution.py:28
  148.7 288.1 %all-reduce.9.cloned.1.call-start = ((), (), s32[]{:S(2)}) async-start(), calls=%async_computation.2 | async-start | bytes 2097152 | tf_op jit(solution)/shard_map/psum | solution.py:23
  307.4 256.6 %all-reduce.11.cloned.1.call-start = ((), (), s32[]{:S(2)}) async-start(), calls=%async_computation.3 | async-start | bytes 131072 | tf_op jit(solution)/shard_map/psum | solution.py:28
Sparse Core Ops, SparseCore 0:
  13.2 131.9 all-reduce.4
  151.3 121.1 all-reduce.6
  307.5 129.2 all-reduce.8
  442.8 121.1 all-reduce.10
where the time goes:
time: 608 us; the launch traced here: 607 us
  waiting for transfers between devices  510 us (84%)
  other arithmetic  59.2 us (10%)
  matrix products  15.8 us (3%)
  between operations  13.8 us (2%)
  local copies, waits for them, and re-layouts  8.45 us (1%)
    psum x2, waiting for transfers between devices, per_device(): summed = lax.psum(partial_sum, ('gx', 'gy', 'gz'))  262 us
    psum x2, waiting for transfers between devices, per_device(): gram = lax.psum(gram_local, ('gx', 'gy', 'gz'))  247 us
    another operation x6, other arithmetic, per_device(): lower_tri = jnp.linalg.cholesky(gram)  29.4 us
    another operation x3, other arithmetic, per_device(): lax.linalg.triangular_solve(lower_tri, projected, left_side=False, lower=...  24.7 us
  transfers between devices with their start and end apart: 4, of which 4 were waited for; matrix products, arithmetic and copies ran while one was open for 0% of the time, Pallas kernels for 0%

commit v1 on v0

v1 whole, which is shorter than its diff:
```python
import functools
import math

import jax
import jax.numpy as jnp
from jax import lax
from jax.experimental import pallas as pl
from jax.experimental.pallas import tpu as pltpu
from jax.sharding import PartitionSpec as P

POWER = 2
AXES = ("gx", "gy", "gz")
MESH = pl.DeviceIdType.MESH
HIGHEST = lax.Precision.HIGHEST
PANEL = 8


def plan(sizes, days):
    size_x, size_y, size_z = sizes
    plane = (size_x // 2) * size_z
    line = size_y
    half = days // 2
    block = half // plane
    scatter = block % (16 * line) == 0
    piece = block // line if scatter else block
    return plane, line, half, block, scatter, piece


def step_kernel(
    sizes, units, o_ref, c_ref, p_ref, g_ref,
    ct, s_send, s_recv, s_mine, x_recv, z_sum, z_recv, w,
    g_loc, g_recv, g_half, gx_recv, g_plane, gz_recv, g_full,
    c_ss, c_rs, x_ss, x_rs, z_ss, z_rs, az_ss, az_rs, ax_ss, ax_rs, ac_ss, ac_rs,
    gc_ss, gc_rs, gx_ss, gx_rs, gz_ss, gz_rs, gf_ss, gf_rs,
):
    days = o_ref.shape[1]
    rows = o_ref.shape[0]
    rank = c_ref.shape[1]
    plane, line, half, block, scatter, piece = plan(sizes, days)
    size_z = sizes[2]
    ix, iy, iz = (lax.axis_index(a) for a in AXES)
    core = lax.rem(ix, 2)
    q = lax.div(ix, 2) * size_z + iz
    z = iy

    def device(c_at, q_at, z_at):
        return (lax.div(q_at, size_z) * 2 + c_at, z_at, lax.rem(q_at, size_z))

    other = 1 - core
    pair_dev = device(other, q, z)

    def q_to(k):
        return lax.rem(q + k, plane)

    def q_from(k):
        return lax.rem(q + plane - k, plane)

    def z_to(k):
        return lax.rem(z + k, line)

    def z_from(k):
        return lax.rem(z + line - k, line)

    def remote(src, dst, ss, rs, dev):
        return pltpu.make_async_remote_copy(
            src_ref=src, dst_ref=dst, send_sem=ss, recv_sem=rs, device_id=dev, device_id_type=MESH
        )

    partners = [pair_dev]
    partners += [device(core, q_to(k), z) for k in range(1, plane)]
    partners += [device(core, q, z_to(k)) for k in range(1, line)]
    barrier = pltpu.get_barrier_semaphore()
    for dev in partners:
        pl.semaphore_signal(barrier, inc=1, device_id=dev, device_id_type=MESH)

    ct[...] = c_ref[...].astype(jnp.float32).T.astype(jnp.bfloat16)

    def product(dst, side, first, width):
        at = pl.multiple_of(side * half + first, 128)
        part = jnp.dot(ct[...], o_ref[:, pl.ds(at, width)], preferred_element_type=jnp.float32)
        dst[pl.ds(pl.multiple_of(first, 128), width), :] = part.T

    by_block = block % 128 == 0
    sends = []
    order = list(range(1, plane)) + [0]
    if not by_block:
        for first in range(0, half, 256):
            product(s_send, other, first, min(256, half))

    def q_rows(k):
        return pl.multiple_of(q_to(k) * block, block)

    for n, k in enumerate(order):
        at = q_rows(k)
        if by_block:
            product(s_send, other, at, block)
        if n == 0:
            pl.semaphore_wait(barrier, len(partners))
        copy = remote(
            s_send.at[pl.ds(at, block)], s_recv.at[pl.ds(at, block)], c_ss.at[k], c_rs.at[k], pair_dev
        )
        copy.start()
        sends.append(copy)
    if not by_block:
        for first in range(0, half, 256):
            product(s_mine, core, first, min(256, half))
    for k in order:
        at = q_rows(k)
        if by_block:
            product(s_mine, core, at, block)
        mine = s_recv.at[pl.ds(at, block)]
        remote(mine, mine, c_ss.at[k], c_rs.at[k], pair_dev).wait_recv()
        if k:
            s_mine[pl.ds(at, block), :] += s_recv[pl.ds(at, block), :]
            copy = remote(
                s_mine.at[pl.ds(at, block)], x_recv.at[k - 1], x_ss.at[k - 1], x_rs.at[k - 1],
                device(core, q_to(k), z),
            )
            copy.start()
            sends.append(copy)
    own = q_rows(0)
    z_sum[...] = s_mine[pl.ds(own, block), :] + s_recv[pl.ds(own, block), :]
    for k in range(1, plane):
        remote(x_recv.at[k - 1], x_recv.at[k - 1], x_ss.at[k - 1], x_rs.at[k - 1], pair_dev).wait_recv()
        z_sum[...] += x_recv[k - 1]

    for k in range(1, line):
        first = pl.multiple_of(z_to(k) * piece, piece) if scatter else 0
        copy = remote(
            z_sum.at[pl.ds(first, piece)], z_recv.at[k - 1], z_ss.at[k - 1], z_rs.at[k - 1],
            device(core, q, z_to(k)),
        )
        copy.start()
        sends.append(copy)
    first = pl.multiple_of(z * piece, piece) if scatter else 0
    total = z_sum[pl.ds(first, piece), :]
    for k in range(1, line):
        remote(z_recv.at[k - 1], z_recv.at[k - 1], z_ss.at[k - 1], z_rs.at[k - 1], pair_dev).wait_recv()
        total = total + z_recv[k - 1]

    pieces = line if scatter else 1

    def w_rows(side, q_at, z_at):
        at = side * half + q_at * block + (z_at * piece if scatter else 0)
        return w.at[pl.ds(pl.multiple_of(at, piece), piece)]

    at = core * half + q * block + (z * piece if scatter else 0)
    w[pl.ds(pl.multiple_of(at, piece), piece), :] = (total * (1.0 / math.sqrt(units))).astype(jnp.bfloat16)

    def start(ref, ss, rs, dev):
        copy = remote(ref, ref, ss, rs, dev)
        copy.start()
        sends.append(copy)

    mine = w_rows(core, q, z)
    for k in range(1, pieces):
        start(mine, az_ss.at[k], az_rs.at[k], device(core, q, z_to(k)))
    for kz in range(pieces):
        mine = w_rows(core, q, z_from(kz))
        if kz:
            remote(mine, mine, az_ss.at[kz], az_rs.at[kz], pair_dev).wait_recv()
        for k in range(1, plane):
            start(mine, ax_ss.at[kz, k], ax_rs.at[kz, k], device(core, q_to(k), z))
        start(mine, ac_ss.at[kz, 0], ac_rs.at[kz, 0], pair_dev)
    for kz in range(pieces):
        for k in range(1, plane):
            mine = w_rows(core, q_from(k), z_from(kz))
            remote(mine, mine, ax_ss.at[kz, k], ax_rs.at[kz, k], pair_dev).wait_recv()
            start(mine, ac_ss.at[kz, k], ac_rs.at[kz, k], pair_dev)
    for kz in range(pieces):
        for k in range(plane):
            mine = w_rows(other, q_from(k), z_from(kz))
            remote(mine, mine, ac_ss.at[kz, k], ac_rs.at[kz, k], pair_dev).wait_recv()

    tile = 256 if rows % 256 == 0 else rows
    for first in range(0, rows, tile):
        part = jnp.dot(o_ref[first:first + tile, :], w[...], preferred_element_type=jnp.float32)
        p_ref[first:first + tile, :] = part * (1.0 / math.sqrt(days))
    projected = p_ref[...]
    g_loc[...] = jnp.dot(
        projected.T, projected, precision=HIGHEST, preferred_element_type=jnp.float32
    ) * (1.0 / units)

    gh = rank // 2
    mine_at = pl.multiple_of(core * gh, gh)
    other_at = pl.multiple_of(other * gh, gh)
    copy = remote(g_loc.at[pl.ds(other_at, gh)], g_recv, gc_ss, gc_rs, pair_dev)
    copy.start()
    sends.append(copy)
    copy.wait_recv()
    g_half[...] = g_loc[pl.ds(mine_at, gh), :] + g_recv[...]
    for k in range(1, plane):
        copy = remote(
            g_half, gx_recv.at[q], gx_ss.at[k], gx_rs.at[k], device(core, q_to(k), z)
        )
        copy.start()
        sends.append(copy)
    gx_recv[q] = g_half[...]
    for k in range(1, plane):
        slot = gx_recv.at[q_from(k)]
        remote(slot, slot, gx_ss.at[k], gx_rs.at[k], pair_dev).wait_recv()
    total = gx_recv[0]
    for k in range(1, plane):
        total = total + gx_recv[k]
    g_plane[...] = total
    for k in range(1, line):
        copy = remote(g_plane, gz_recv.at[z], gz_ss.at[k], gz_rs.at[k], device(core, q, z_to(k)))
        copy.start()
        sends.append(copy)
    gz_recv[z] = total
    for k in range(1, line):
        slot = gz_recv.at[z_from(k)]
        remote(slot, slot, gz_ss.at[k], gz_rs.at[k], pair_dev).wait_recv()
    total = gz_recv[0]
    for k in range(1, line):
        total = total + gz_recv[k]
    g_full[pl.ds(mine_at, gh), :] = total
    mine = g_full.at[pl.ds(mine_at, gh)]
    copy = remote(mine, mine, gf_ss, gf_rs, pair_dev)
    copy.start()
    sends.append(copy)
    theirs = g_full.at[pl.ds(other_at, gh)]
    remote(theirs, theirs, gf_ss, gf_rs, pair_dev).wait_recv()
    g_ref[...] = g_full[...]
    for copy in sends:
        copy.wait_send()


def step(sizes, units, outcomes, current):
    rows, days = outcomes.shape
    rank = current.shape[1]
    plane, line, half, block, scatter, piece = plan(sizes, days)
    pieces = line if scatter else 1
    gh = rank // 2
    f32, bf16 = jnp.float32, jnp.bfloat16
    dma = pltpu.SemaphoreType.DMA
    vmem = pl.BlockSpec(memory_space=pltpu.VMEM)
    pair = lambda *n: [dma(n), dma(n)]
    return pl.pallas_call(
        functools.partial(step_kernel, sizes, units),
        out_shape=(
            jax.ShapeDtypeStruct((rows, rank), f32),
            jax.ShapeDtypeStruct((rank, rank), f32),
        ),
        in_specs=[vmem, vmem],
        out_specs=(vmem, vmem),
        scratch_shapes=[
            pltpu.VMEM((rank, rows), bf16),
            pltpu.VMEM((half, rank), f32),
            pltpu.VMEM((half, rank), f32),
            pltpu.VMEM((half, rank), f32),
            pltpu.VMEM((max(plane - 1, 1), block, rank), f32),
            pltpu.VMEM((block, rank), f32),
            pltpu.VMEM((max(line - 1, 1), piece, rank), f32),
            pltpu.VMEM((days, rank), bf16),
            pltpu.VMEM((rank, rank), f32),
            pltpu.VMEM((gh, rank), f32),
            pltpu.VMEM((gh, rank), f32),
            pltpu.VMEM((plane, gh, rank), f32),
            pltpu.VMEM((gh, rank), f32),
            pltpu.VMEM((line, gh, rank), f32),
            pltpu.VMEM((rank, rank), f32),
            *pair(plane), *pair(plane), *pair(line), *pair(line),
            *pair(pieces, plane), *pair(pieces, plane),
            dma, dma, *pair(plane), *pair(line), dma, dma,
        ],
        compiler_params=pltpu.CompilerParams(
            collective_id=0, has_side_effects=True, vmem_limit_bytes=48 * 1024 * 1024
        ),
        name="power_step",
    )(outcomes, current)


def sharp_rsqrt(x):
    r = lax.rsqrt(x)
    return r * (1.5 - 0.5 * ((x * r) * r))


def factor_kernel(p_ref, g_ref, q_ref, r_ref, inv_ref):
    rank = g_ref.shape[0]
    count = rank // PANEL
    row_at = lax.broadcasted_iota(jnp.int32, (PANEL, rank), 0)
    col_at = lax.broadcasted_iota(jnp.int32, (PANEL, rank), 1)
    left = [g_ref[k * PANEL:(k + 1) * PANEL, :] for k in range(count)]
    right = [jnp.where(col_at == row_at + k * PANEL, 1.0, 0.0) for k in range(count)]
    for k in range(count):
        a, b = left[k], right[k]
        cols = [
            jnp.broadcast_to(a[:, k * PANEL + j:k * PANEL + j + 1], (PANEL, rank)) for j in range(PANEL)
        ]
        for j in range(PANEL):
            scale = sharp_rsqrt(jnp.broadcast_to(cols[j][j:j + 1, :], (PANEL, rank)))
            low = jnp.where(row_at > j, cols[j] * scale, 0.0)
            for m in range(j + 1, PANEL):
                cols[m] = cols[m] - low * jnp.broadcast_to(low[m:m + 1, :], (PANEL, rank))
            a_row = jnp.broadcast_to(a[j:j + 1, :], (PANEL, rank)) * scale
            b_row = jnp.broadcast_to(b[j:j + 1, :], (PANEL, rank)) * scale
            here = row_at == j
            a = jnp.where(here, a_row, a - low * a_row)
            b = jnp.where(here, b_row, b - low * b_row)
        r_ref[k * PANEL:(k + 1) * PANEL, :] = jnp.where(col_at >= row_at + k * PANEL, a, 0.0)
        inv_ref[k * PANEL:(k + 1) * PANEL, :] = b
        if k + 1 < count:
            both = jnp.concatenate([a, b], axis=1)
            down = lax.dot_general(
                a, both, (((0,), (0,)), ((), ())), precision=HIGHEST, preferred_element_type=jnp.float32
            )
            for m in range(k + 1, count):
                left[m] = left[m] - down[m * PANEL:(m + 1) * PANEL, :rank]
                right[m] = right[m] - down[m * PANEL:(m + 1) * PANEL, rank:]
    q_ref[...] = lax.dot_general(
        p_ref[...], inv_ref[...], (((1,), (1,)), ((), ())), precision=HIGHEST,
        preferred_element_type=jnp.float32,
    ).astype(q_ref.dtype)


def orthonormalize(projected, gram, dtype):
    rank = gram.shape[0]
    vmem = pl.BlockSpec(memory_space=pltpu.VMEM)
    return pl.pallas_call(
        factor_kernel,
        out_shape=(
            jax.ShapeDtypeStruct(projected.shape, dtype),
            jax.ShapeDtypeStruct((rank, rank), jnp.float32),
        ),
        in_specs=[vmem, vmem],
        out_specs=(vmem, vmem),
        scratch_shapes=[pltpu.VMEM((rank, rank), jnp.float32)],
        name="orthonormalize",
    )(projected, gram)


def per_device(sizes, outcomes, sketch):
    units = outcomes.shape[0] * math.prod(sizes)
    current = sketch
    for power_step in range(POWER):
        last = power_step == POWER - 1
        projected, gram = step(sizes, units, outcomes, current)
        current, factor = orthonormalize(projected, gram, jnp.float32 if last else jnp.bfloat16)
    return current, factor


def solution(mesh):
    return jax.shard_map(
        functools.partial(per_device, tuple(mesh.shape[a] for a in AXES)),
        mesh=mesh,
        in_specs=(P(AXES, None), P(AXES, None)),
        out_specs=(P(AXES, None), P()),
        check_vma=False,
    )
```

time: 608 us -> 106 us (0.17)
  waiting for transfers between devices: 510 us -> 0 us
  Pallas kernels: 0 us -> 98.8 us
  other arithmetic: 59.2 us -> 0 us
  matrix products: 15.8 us -> 0 us
  between operations: 13.8 us -> 0.68 us
    psum x4 -> x0, waiting for transfers between devices: 510 us -> none  [the longest x2 262 us: per_device(): summed = lax.psum(partial_sum, ('gx', 'gy', 'gz'))]
    pallas_call x0 -> x4, Pallas kernels: none -> 98.8 us  [the longest x2 75.5 us: step(): pl.pallas_call(functools.partial(step_kernel, sizes, units), out_shape=(j...]
    another operation x9 -> x0, other arithmetic: 54.1 us -> none  [the longest x6 29.4 us: per_device(): lower_tri = jnp.linalg.cholesky(gram)]
    dot_general x6 -> x0, matrix products: 12.4 us -> none  [the longest x2 5.35 us: per_device(): lax.dot_general(outcomes, current, (((0,), (0,)), ((), ())), preferred_el...]
  transfers between devices with their start and end apart: 4 -> 0, of which waited for: 4 -> 0; matrix products, arithmetic and copies ran while one was open for 0% -> 0% of each run, Pallas kernels for 0% -> 0%
where the time goes in v1:
time: 106 us
  Pallas kernels  98.8 us (93%)
  local copies, waits for them, and re-layouts  6.47 us (6%)
    pallas_call x2, Pallas kernels, step(): pl.pallas_call(functools.partial(step_kernel, sizes, units), out_shape=(j...  75.5 us
    pallas_call x2, Pallas kernels, orthonormalize(): pl.pallas_call(factor_kernel, out_shape=(jax.ShapeDtypeStruct(projected.s...  23.3 us
    unnamed x16, local copies, waits for them, and re-layouts  6.47 us

profile of v1, /device:TPU:1, one launch (start us, length us, event | category | flops | bytes accessed | tf_op | source)
XLA Modules:
  0.0 105.9 jit_solution(7067874084846181452)
XLA Ops:
  0.6 0.0 copy-start
  0.6 1.9 %copy-done = bf16[768,2048]{1,0:T(8,128)(2,1)S(1)} copy-done((bf16[768,2048]{1,0:T(8,128)(2,1)S(1)}, bf16[768,2048]{1,0:T(8,128)(2,1)}, u32[]{:S(2)}) %copy-start) | copy-done | bytes 3145752
  2.5 0.0 copy-start.4
  2.5 0.9 copy-done.4
  3.4 0.0 copy-start.1
  3.4 38.7 %power_step.2 = (f32[768,128]{1,0:T(8,128)S(1)}, f32[128,128]{1,0:T(8,128)S(1)}) custom-call(bf16[768,2048]{1,0:T(8,128)(2,1)S(1)} %copy-done, bf16[768,128]{1,0:T(8,128)(2,1)S(1)} %copy-done.4), custom_call_target="tpu_custom_call" | custom-call | tf_op jit(solution)/shard_map/power_step/pallas_call | solution.py:239
  42.1 0.0 copy-start.3
  42.1 0.7 copy-done.3
  42.9 0.0 copy-start.7
  42.9 0.6 copy-done.7
  43.5 11.5 %orthonormalize.2 = (bf16[768,128]{1,0:T(8,128)(2,1)}, f32[128,128]{1,0:T(8,128)}) custom-call(f32[768,128]{1,0:T(8,128)} %copy-done.3, f32[128,128]{1,0:T(8,128)} %copy-done.7), custom_call_target="tpu_custom_call" | custom-call | tf_op jit(solution)/shard_map/orthonormalize/pallas_call | solution.py:320
  55.0 0.0 copy-done.1
  55.0 0.0 copy-start.5
  55.0 0.9 copy-done.5
  55.9 36.9 %power_step.3 = (f32[768,128]{1,0:T(8,128)S(1)}, f32[128,128]{1,0:T(8,128)S(1)}) custom-call(bf16[768,2048]{1,0:T(8,128)(2,1)S(1)} %copy-done.1, bf16[768,128]{1,0:T(8,128)(2,1)S(1)} %copy-done.5), custom_call_target="tpu_custom_call" | custom-call | tf_op jit(solution)/shard_map/power_step/pallas_call | solution.py:239
  92.8 0.0 copy-start.2
  92.8 0.7 copy-done.2
  93.6 0.0 copy-start.6
  93.6 0.6 copy-done.6
  94.2 11.8 %orthonormalize.3 = (f32[768,128]{1,0:T(8,128)}, f32[128,128]{1,0:T(8,128)}) custom-call(f32[768,128]{1,0:T(8,128)} %copy-done.2, f32[128,128]{1,0:T(8,128)} %copy-done.6), custom_call_target="tpu_custom_call" | custom-call | tf_op jit(solution)/shard_map/orthonormalize/pallas_call | solution.py:320
Async XLA Ops:
  0.6 1.9 %copy-start = (bf16[768,2048]{1,0:T(8,128)(2,1)S(1)}, bf16[768,2048]{1,0:T(8,128)(2,1)}, u32[]{:S(2)}) copy-start(bf16[768,2048]{1,0:T(8,128)(2,1)} %o_ref.3) | copy-start | bytes 9437188
  2.5 0.9 copy-start.4
  3.4 51.6 %copy-start.1 = (bf16[768,2048]{1,0:T(8,128)(2,1)S(1)}, bf16[768,2048]{1,0:T(8,128)(2,1)}, u32[]{:S(2)}) copy-start(bf16[768,2048]{1,0:T(8,128)(2,1)} %o_ref.3) | copy-start | bytes 9437188
  42.1 0.7 copy-start.3
  42.9 0.6 copy-start.7
  55.0 0.9 copy-start.5
  92.8 0.7 copy-start.2
  93.6 0.6 copy-start.6

commit v2 on v0

v2 whole, which is shorter than its diff:
```python
import functools
import math

import jax
import jax.numpy as jnp
from jax import lax
from jax.experimental import pallas as pl
from jax.experimental.pallas import tpu as pltpu
from jax.sharding import PartitionSpec as P

POWER = 2
AXES = ("gx", "gy", "gz")
MESH = pl.DeviceIdType.MESH
HIGHEST = lax.Precision.HIGHEST
PANEL = 32


def plan(sizes, days):
    size_x, size_y, size_z = sizes
    plane = (size_x // 2) * size_z
    line = size_y
    half = days // 2
    block = half // plane
    scatter = block % (16 * line) == 0
    piece = block // line if scatter else block
    return plane, line, half, block, scatter, piece


def sharp_rsqrt(x):
    r = lax.rsqrt(x)
    return r * (1.5 - 0.5 * ((x * r) * r))


def factorize(g_ref, r_ref, inv_ref):
    rank = g_ref.shape[0]
    count = rank // PANEL
    row_at = lax.broadcasted_iota(jnp.int32, (PANEL, rank), 0)
    col_at = lax.broadcasted_iota(jnp.int32, (PANEL, rank), 1)
    left = [g_ref[k * PANEL:(k + 1) * PANEL, :] for k in range(count)]
    right = [jnp.where(col_at == row_at + k * PANEL, 1.0, 0.0) for k in range(count)]
    for k in range(count):
        a, b = left[k], right[k]
        cols = [
            jnp.broadcast_to(a[:, k * PANEL + j:k * PANEL + j + 1], (PANEL, rank)) for j in range(PANEL)
        ]
        for j in range(PANEL):
            scale = sharp_rsqrt(jnp.broadcast_to(cols[j][j:j + 1, :], (PANEL, rank)))
            low = jnp.where(row_at > j, cols[j] * scale, 0.0)
            for m in range(j + 1, PANEL):
                cols[m] = cols[m] - low * jnp.broadcast_to(low[m:m + 1, :], (PANEL, rank))
            a_row = jnp.broadcast_to(a[j:j + 1, :], (PANEL, rank)) * scale
            b_row = jnp.broadcast_to(b[j:j + 1, :], (PANEL, rank)) * scale
            here = row_at == j
            a = jnp.where(here, a_row, a - low * a_row)
            b = jnp.where(here, b_row, b - low * b_row)
        if r_ref is not None:
            r_ref[k * PANEL:(k + 1) * PANEL, :] = jnp.where(col_at >= row_at + k * PANEL, a, 0.0)
        inv_ref[k * PANEL:(k + 1) * PANEL, :] = b
        if k + 1 < count:
            both = jnp.concatenate([a, b], axis=1)
            down = lax.dot_general(
                a, both, (((0,), (0,)), ((), ())), precision=HIGHEST, preferred_element_type=jnp.float32
            )
            for m in range(k + 1, count):
                left[m] = left[m] - down[m * PANEL:(m + 1) * PANEL, :rank]
                right[m] = right[m] - down[m * PANEL:(m + 1) * PANEL, rank:]


def times_inverse(x, inv_ref):
    return lax.dot_general(
        x, inv_ref[...], (((1,), (1,)), ((), ())), precision=HIGHEST, preferred_element_type=jnp.float32
    )


def power_kernel(sizes, units, o_hbm, c_ref, q_ref, r_ref, o_ref, o_sem, p_ref, *scratch):
    rows, days = o_ref.shape
    rank = c_ref.shape[1]
    plane, line, half, block, scatter, piece = plan(sizes, days)
    size_z = sizes[2]
    ix, iy, iz = (lax.axis_index(a) for a in AXES)
    core = lax.rem(ix, 2)
    q = lax.div(ix, 2) * size_z + iz
    z = iy

    def device(c_at, q_at, z_at):
        return (lax.div(q_at, size_z) * 2 + c_at, z_at, lax.rem(q_at, size_z))

    other = 1 - core
    pair_dev = device(other, q, z)

    def q_to(k):
        return lax.rem(q + k, plane)

    def q_from(k):
        return lax.rem(q + plane - k, plane)

    def z_to(k):
        return lax.rem(z + k, line)

    def z_from(k):
        return lax.rem(z + line - k, line)

    def remote(src, dst, ss, rs, dev):
        return pltpu.make_async_remote_copy(
            src_ref=src, dst_ref=dst, send_sem=ss, recv_sem=rs, device_id=dev, device_id_type=MESH
        )

    sends = []

    def send(src, dst, ss, rs, dev):
        copy = remote(src, dst, ss, rs, dev)
        copy.start()
        sends.append(copy)

    def arrived(ref, ss, rs):
        remote(ref, ref, ss, rs, pair_dev).wait_recv()

    partners = [pair_dev]
    partners += [device(core, q_to(k), z) for k in range(1, plane)]
    partners += [device(core, q, z_to(k)) for k in range(1, line)]
    barrier = pltpu.get_barrier_semaphore()
    for dev in partners:
        pl.semaphore_signal(barrier, inc=1, device_id=dev, device_id_type=MESH)

    by_block = block % 128 == 0
    order = list(range(1, plane)) + [0]

    def q_rows(k):
        return pl.multiple_of(q_to(k) * block, block)

    def columns(side, first, width):
        return pl.ds(pl.multiple_of(side * half + first, 128), width)

    loads = {}
    if by_block:
        for n, (at_side, k) in enumerate([(1, k) for k in order] + [(0, k) for k in order]):
            cut = columns(other if at_side else core, q_rows(k), block)
            loads[at_side, k] = pltpu.make_async_copy(o_hbm.at[:, cut], o_ref.at[:, cut], o_sem.at[n])
            loads[at_side, k].start()
    else:
        loads[0, 0] = pltpu.make_async_copy(o_hbm, o_ref, o_sem.at[0])
        loads[0, 0].start()
        loads[0, 0].wait()

    per = len(scratch) // POWER
    gram_steps = inverse = p_t = None
    for s in range(POWER):
        (
            ct, s_send, s_recv, s_mine, x_recv, z_sum, z_recv, w,
            g_loc, g_recv, g_half, gx_recv, g_plane, gz_recv, g_full, inv_ref,
            c_ss, c_rs, x_ss, x_rs, z_ss, z_rs, az_ss, az_rs, ax_ss, ax_rs, ac_ss, ac_rs,
            gc_ss, gc_rs, gx_ss, gx_rs, gz_ss, gz_rs, gf_ss, gf_rs,
        ) = scratch[s * per:(s + 1) * per]

        if s == 0:
            ct[:rank, :] = c_ref[...].astype(jnp.float32).T.astype(jnp.bfloat16)
        else:
            high = p_t.astype(jnp.bfloat16)
            ct[:rank, :] = high
            ct[rank:, :] = (p_t - high.astype(jnp.float32)).astype(jnp.bfloat16)

        def product(dst, side, first, width):
            cut = columns(side, first, width)
            now = ct[:rank, :] if s == 0 else ct[...]
            part = jnp.dot(now, o_ref[:, cut], preferred_element_type=jnp.float32)
            if s:
                part = part[:rank] + part[rank:]
            dst[pl.ds(pl.multiple_of(first, 128), width), :] = part.T

        if not by_block:
            for first in range(0, half, 256):
                product(s_send, other, first, min(256, half))
        for n, k in enumerate(order):
            at = q_rows(k)
            if by_block:
                if s == 0:
                    loads[1, k].wait()
                product(s_send, other, at, block)
            if s == 0 and n == 0:
                pl.semaphore_wait(barrier, len(partners))
            send(s_send.at[pl.ds(at, block)], s_recv.at[pl.ds(at, block)], c_ss.at[k], c_rs.at[k], pair_dev)
        if gram_steps:
            gram_steps[0]()
        if not by_block:
            for first in range(0, half, 256):
                product(s_mine, core, first, min(256, half))
        for k in order:
            at = q_rows(k)
            if by_block:
                if s == 0:
                    loads[0, k].wait()
                product(s_mine, core, at, block)
            arrived(s_recv.at[pl.ds(at, block)], c_ss.at[k], c_rs.at[k])
            if k:
                s_mine[pl.ds(at, block), :] += s_recv[pl.ds(at, block), :]
                send(
                    s_mine.at[pl.ds(at, block)], x_recv.at[k - 1], x_ss.at[k - 1], x_rs.at[k - 1],
                    device(core, q_to(k), z),
                )
        if gram_steps:
            gram_steps[1]()
        own = q_rows(0)
        z_sum[...] = s_mine[pl.ds(own, block), :] + s_recv[pl.ds(own, block), :]
        for k in range(1, plane):
            arrived(x_recv.at[k - 1], x_ss.at[k - 1], x_rs.at[k - 1])
            z_sum[...] += x_recv[k - 1]

        for k in range(1, line):
            first = pl.multiple_of(z_to(k) * piece, piece) if scatter else 0
            send(
                z_sum.at[pl.ds(first, piece)], z_recv.at[k - 1], z_ss.at[k - 1], z_rs.at[k - 1],
                device(core, q, z_to(k)),
            )
        if gram_steps:
            gram_steps[2]()
            gram_steps[3]()
            factorize(gram_steps[4], None, inverse)
        first = pl.multiple_of(z * piece, piece) if scatter else 0
        total = z_sum[pl.ds(first, piece), :]
        for k in range(1, line):
            arrived(z_recv.at[k - 1], z_ss.at[k - 1], z_rs.at[k - 1])
            total = total + z_recv[k - 1]
        total = total * (1.0 / math.sqrt(units))
        if inverse is not None:
            total = times_inverse(total, inverse)

        pieces = line if scatter else 1

        def w_rows(side, q_at, z_at):
            at = side * half + q_at * block + (z_at * piece if scatter else 0)
            return w.at[pl.ds(pl.multiple_of(at, piece), piece)]

        at = core * half + q * block + (z * piece if scatter else 0)
        w[pl.ds(pl.multiple_of(at, piece), piece), :] = total.astype(jnp.bfloat16)

        mine = w_rows(core, q, z)
        for k in range(1, pieces):
            send(mine, mine, az_ss.at[k], az_rs.at[k], device(core, q, z_to(k)))
        for kz in range(pieces):
            mine = w_rows(core, q, z_from(kz))
            if kz:
                arrived(mine, az_ss.at[kz], az_rs.at[kz])
            for k in range(1, plane):
                send(mine, mine, ax_ss.at[kz, k], ax_rs.at[kz, k], device(core, q_to(k), z))
            send(mine, mine, ac_ss.at[kz, 0], ac_rs.at[kz, 0], pair_dev)
        for kz in range(pieces):
            for k in range(1, plane):
                mine = w_rows(core, q_from(k), z_from(kz))
                arrived(mine, ax_ss.at[kz, k], ax_rs.at[kz, k])
                send(mine, mine, ac_ss.at[kz, k], ac_rs.at[kz, k], pair_dev)
        for kz in range(pieces):
            for k in range(plane):
                arrived(w_rows(other, q_from(k), z_from(kz)), ac_ss.at[kz, k], ac_rs.at[kz, k])

        tile = 256 if rows % 256 == 0 else rows
        for first in range(0, rows, tile):
            part = jnp.dot(o_ref[first:first + tile, :], w[...], preferred_element_type=jnp.float32)
            p_ref[first:first + tile, :] = part * (1.0 / math.sqrt(days))
        projected = p_ref[...]
        p_t = projected.T
        g_loc[...] = jnp.dot(
            p_t, projected, precision=HIGHEST, preferred_element_type=jnp.float32
        ) * (1.0 / units)

        gh = rank // 2
        mine_at = pl.multiple_of(core * gh, gh)
        other_at = pl.multiple_of(other * gh, gh)
        send(g_loc.at[pl.ds(other_at, gh)], g_recv, gc_ss.at[0], gc_rs.at[0], pair_dev)

        def gram_plane_out(g_recv=g_recv, gc_ss=gc_ss, gc_rs=gc_rs, g_half=g_half, g_loc=g_loc,
                           gx_recv=gx_recv, gx_ss=gx_ss, gx_rs=gx_rs):
            arrived(g_recv, gc_ss.at[0], gc_rs.at[0])
            g_half[...] = g_loc[pl.ds(mine_at, gh), :] + g_recv[...]
            for k in range(1, plane):
                send(g_half, gx_recv.at[q], gx_ss.at[k], gx_rs.at[k], device(core, q_to(k), z))

        def gram_line_out(g_half=g_half, gx_recv=gx_recv, gx_ss=gx_ss, gx_rs=gx_rs, g_plane=g_plane,
                          gz_recv=gz_recv, gz_ss=gz_ss, gz_rs=gz_rs):
            gx_recv[q] = g_half[...]
            for k in range(1, plane):
                arrived(gx_recv.at[q_from(k)], gx_ss.at[k], gx_rs.at[k])
            total = gx_recv[0]
            for k in range(1, plane):
                total = total + gx_recv[k]
            g_plane[...] = total
            for k in range(1, line):
                send(g_plane, gz_recv.at[z], gz_ss.at[k], gz_rs.at[k], device(core, q, z_to(k)))

        def gram_pair_out(g_plane=g_plane, gz_recv=gz_recv, gz_ss=gz_ss, gz_rs=gz_rs, g_full=g_full,
                          gf_ss=gf_ss, gf_rs=gf_rs):
            gz_recv[z] = g_plane[...]
            for k in range(1, line):
                arrived(gz_recv.at[z_from(k)], gz_ss.at[k], gz_rs.at[k])
            total = gz_recv[0]
            for k in range(1, line):
                total = total + gz_recv[k]
            g_full[pl.ds(mine_at, gh), :] = total
            mine = g_full.at[pl.ds(mine_at, gh)]
            send(mine, mine, gf_ss.at[0], gf_rs.at[0], pair_dev)

        def gram_done(g_full=g_full, gf_ss=gf_ss, gf_rs=gf_rs):
            arrived(g_full.at[pl.ds(other_at, gh)], gf_ss.at[0], gf_rs.at[0])

        gram_steps = (gram_plane_out, gram_line_out, gram_pair_out, gram_done, g_full)
        inverse = inv_ref

    for part in gram_steps[:4]:
        part()
    factorize(gram_steps[4], r_ref, inverse)
    q_ref[...] = times_inverse(p_ref[...], inverse)
    for copy in sends:
        copy.wait_send()


def per_device(sizes, outcomes, sketch):
    rows, days = outcomes.shape
    rank = sketch.shape[1]
    units = rows * math.prod(sizes)
    plane, line, half, block, scatter, piece = plan(sizes, days)
    pieces = line if scatter else 1
    gh = rank // 2
    f32, bf16 = jnp.float32, jnp.bfloat16
    dma = pltpu.SemaphoreType.DMA
    vmem = pl.BlockSpec(memory_space=pltpu.VMEM)
    pair = lambda *n: [dma(n), dma(n)]
    one_step = [
        pltpu.VMEM((2 * rank, rows), bf16),
        pltpu.VMEM((half, rank), f32),
        pltpu.VMEM((half, rank), f32),
        pltpu.VMEM((half, rank), f32),
        pltpu.VMEM((max(plane - 1, 1), block, rank), f32),
        pltpu.VMEM((block, rank), f32),
        pltpu.VMEM((max(line - 1, 1), piece, rank), f32),
        pltpu.VMEM((days, rank), bf16),
        pltpu.VMEM((rank, rank), f32),
        pltpu.VMEM((gh, rank), f32),
        pltpu.VMEM((gh, rank), f32),
        pltpu.VMEM((plane, gh, rank), f32),
        pltpu.VMEM((gh, rank), f32),
        pltpu.VMEM((line, gh, rank), f32),
        pltpu.VMEM((rank, rank), f32),
        pltpu.VMEM((rank, rank), f32),
        *pair(plane), *pair(plane), *pair(line), *pair(line),
        *pair(pieces, plane), *pair(pieces, plane),
        *pair(1), *pair(plane), *pair(line), *pair(1),
    ]
    return pl.pallas_call(
        functools.partial(power_kernel, sizes, units),
        out_shape=(
            jax.ShapeDtypeStruct((rows, rank), f32),
            jax.ShapeDtypeStruct((rank, rank), f32),
        ),
        in_specs=[pl.BlockSpec(memory_space=pltpu.HBM), vmem],
        out_specs=(vmem, vmem),
        scratch_shapes=[
            pltpu.VMEM((rows, days), bf16),
            dma((2 * plane,)),
            pltpu.VMEM((rows, rank), f32),
            *(one_step * POWER),
        ],
        compiler_params=pltpu.CompilerParams(
            collective_id=0, has_side_effects=True, vmem_limit_bytes=48 * 1024 * 1024
        ),
        name="power_steps",
    )(outcomes, sketch)


def solution(mesh):
    return jax.shard_map(
        functools.partial(per_device, tuple(mesh.shape[a] for a in AXES)),
        mesh=mesh,
        in_specs=(P(AXES, None), P(AXES, None)),
        out_specs=(P(AXES, None), P()),
        check_vma=False,
    )
```

time: 608 us -> 75.9 us (0.12)
  waiting for transfers between devices: 510 us -> 0 us
  Pallas kernels: 0 us -> 70.9 us
  other arithmetic: 59.2 us -> 0 us
  matrix products: 15.8 us -> 0 us
  between operations: 13.8 us -> 0.65 us
    psum x4 -> x0, waiting for transfers between devices: 510 us -> none  [the longest x2 262 us: per_device(): summed = lax.psum(partial_sum, ('gx', 'gy', 'gz'))]
    pallas_call x0 -> x1, Pallas kernels: none -> 70.9 us  [per_device(): pl.pallas_call(functools.partial(power_kernel, sizes, units), out_shape=(...]
    another operation x9 -> x0, other arithmetic: 54.1 us -> none  [the longest x6 29.4 us: per_device(): lower_tri = jnp.linalg.cholesky(gram)]
    dot_general x6 -> x0, matrix products: 12.4 us -> none  [the longest x2 5.35 us: per_device(): lax.dot_general(outcomes, current, (((0,), (0,)), ((), ())), preferred_el...]
  transfers between devices with their start and end apart: 4 -> 0, of which waited for: 4 -> 0; matrix products, arithmetic and copies ran while one was open for 0% -> 0% of each run, Pallas kernels for 0% -> 0%
where the time goes in v2:
time: 75.9 us; the launch traced here: 75.7 us
  Pallas kernels  70.9 us (93%)
  local copies, waits for them, and re-layouts  4.19 us (6%)
    pallas_call x1, Pallas kernels, per_device(): pl.pallas_call(functools.partial(power_kernel, sizes, units), out_shape=(...  70.9 us
    unnamed x6, local copies, waits for them, and re-layouts  4.19 us

profile of v2, /device:TPU:1, one launch (start us, length us, event | category | flops | bytes accessed | tf_op | source)
XLA Modules:
  0.0 75.7 jit_solution(15447921947805745956)
XLA Ops:
  0.6 0.0 copy-start
  0.6 1.9 %copy-done = bf16[768,2048]{1,0:T(8,128)(2,1)S(1)} copy-done((bf16[768,2048]{1,0:T(8,128)(2,1)S(1)}, bf16[768,2048]{1,0:T(8,128)(2,1)}, u32[]{:S(2)}) %copy-start) | copy-done | bytes 3145752
  2.5 0.0 copy-start.1
  2.5 0.9 %copy-done.1 = bf16[768,128]{1,0:T(8,128)(2,1)S(1)} copy-done((bf16[768,128]{1,0:T(8,128)(2,1)S(1)}, bf16[768,128]{1,0:T(8,128)(2,1)}, u32[]{:S(2)}) %copy-start.1) | copy-done | bytes 196632
  3.4 70.9 %power_steps.1 = (f32[768,128]{1,0:T(8,128)S(1)}, f32[128,128]{1,0:T(8,128)S(1)}) custom-call(bf16[768,2048]{1,0:T(8,128)(2,1)S(1)} %copy-done, bf16[768,128]{1,0:T(8,128)(2,1)S(1)} %copy-done.1), custom_call_target="tpu_custom_call" | custom-call | tf_op jit(solution)/shard_map/power_steps/pallas_call | solution.py:347
  74.4 0.7 copy.6
  75.1 0.6 copy.7
Async XLA Ops:
  0.6 1.9 %copy-start = (bf16[768,2048]{1,0:T(8,128)(2,1)S(1)}, bf16[768,2048]{1,0:T(8,128)(2,1)}, u32[]{:S(2)}) copy-start(bf16[768,2048]{1,0:T(8,128)(2,1)} %o_hbm.1) | copy-start | bytes 9437188
  2.5 0.9 %copy-start.1 = (bf16[768,128]{1,0:T(8,128)(2,1)S(1)}, bf16[768,128]{1,0:T(8,128)(2,1)}, u32[]{:S(2)}) copy-start(bf16[768,128]{1,0:T(8,128)(2,1)} %c_ref.1) | copy-start | bytes 589828

commit v3 on v2

--- a/solution.py
+++ b/solution.py
@@ -24,11 +24,6 @@
     scatter = block % (16 * line) == 0
     piece = block // line if scatter else block
     return plane, line, half, block, scatter, piece
-
-
-def sharp_rsqrt(x):
-    r = lax.rsqrt(x)
-    return r * (1.5 - 0.5 * ((x * r) * r))
 
 
 def factorize(g_ref, r_ref, inv_ref):
@@ -43,16 +38,20 @@
         cols = [
             jnp.broadcast_to(a[:, k * PANEL + j:k * PANEL + j + 1], (PANEL, rank)) for j in range(PANEL)
         ]
+        scales = jnp.zeros((PANEL, rank), jnp.float32)
         for j in range(PANEL):
-            scale = sharp_rsqrt(jnp.broadcast_to(cols[j][j:j + 1, :], (PANEL, rank)))
-            low = jnp.where(row_at > j, cols[j] * scale, 0.0)
+            pivot = jnp.broadcast_to(cols[j][j:j + 1, :], (PANEL, rank))
+            root = lax.rsqrt(pivot)
+            inv = root * root
+            inv = inv * (2.0 - pivot * inv)
+            below = jnp.where(row_at > j, cols[j], 0.0)
+            low = below * inv
             for m in range(j + 1, PANEL):
-                cols[m] = cols[m] - low * jnp.broadcast_to(low[m:m + 1, :], (PANEL, rank))
-            a_row = jnp.broadcast_to(a[j:j + 1, :], (PANEL, rank)) * scale
-            b_row = jnp.broadcast_to(b[j:j + 1, :], (PANEL, rank)) * scale
-            here = row_at == j
-            a = jnp.where(here, a_row, a - low * a_row)
-            b = jnp.where(here, b_row, b - low * b_row)
+                cols[m] = cols[m] - low * jnp.broadcast_to(cols[j][m:m + 1, :], (PANEL, rank))
+            scales = jnp.where(row_at == j, root * (1.5 - 0.5 * ((pivot * root) * root)), scales)
+            a = a - low * jnp.broadcast_to(a[j:j + 1, :], (PANEL, rank))
+            b = b - low * jnp.broadcast_to(b[j:j + 1, :], (PANEL, rank))
+        a, b = a * scales, b * scales
         if r_ref is not None:
             r_ref[k * PANEL:(k + 1) * PANEL, :] = jnp.where(col_at >= row_at + k * PANEL, a, 0.0)
         inv_ref[k * PANEL:(k + 1) * PANEL, :] = b
@@ -131,9 +130,13 @@
     def columns(side, first, width):
         return pl.ds(pl.multiple_of(side * half + first, 128), width)
 
+    turns = [(1, order[0])]
+    for n in range(1, plane):
+        turns += [(1, order[n]), (0, order[n - 1])]
+    turns += [(0, order[-1])]
     loads = {}
     if by_block:
-        for n, (at_side, k) in enumerate([(1, k) for k in order] + [(0, k) for k in order]):
+        for n, (at_side, k) in enumerate(turns):
             cut = columns(other if at_side else core, q_rows(k), block)
             loads[at_side, k] = pltpu.make_async_copy(o_hbm.at[:, cut], o_ref.at[:, cut], o_sem.at[n])
             loads[at_side, k].start()
@@ -170,33 +173,29 @@
         if not by_block:
             for first in range(0, half, 256):
                 product(s_send, other, first, min(256, half))
-        for n, k in enumerate(order):
+                product(s_mine, core, first, min(256, half))
+        for n, (at_side, k) in enumerate(turns):
             at = q_rows(k)
             if by_block:
                 if s == 0:
-                    loads[1, k].wait()
-                product(s_send, other, at, block)
+                    loads[at_side, k].wait()
+                product(s_send if at_side else s_mine, other if at_side else core, at, block)
             if s == 0 and n == 0:
                 pl.semaphore_wait(barrier, len(partners))
-            send(s_send.at[pl.ds(at, block)], s_recv.at[pl.ds(at, block)], c_ss.at[k], c_rs.at[k], pair_dev)
-        if gram_steps:
-            gram_steps[0]()
-        if not by_block:
-            for first in range(0, half, 256):
-                product(s_mine, core, first, min(256, half))
-        for k in order:
-            at = q_rows(k)
-            if by_block:
-                if s == 0:
-                    loads[0, k].wait()
-                product(s_mine, core, at, block)
-            arrived(s_recv.at[pl.ds(at, block)], c_ss.at[k], c_rs.at[k])
-            if k:
-                s_mine[pl.ds(at, block), :] += s_recv[pl.ds(at, block), :]
+            if at_side:
                 send(
-                    s_mine.at[pl.ds(at, block)], x_recv.at[k - 1], x_ss.at[k - 1], x_rs.at[k - 1],
-                    device(core, q_to(k), z),
+                    s_send.at[pl.ds(at, block)], s_recv.at[pl.ds(at, block)], c_ss.at[k], c_rs.at[k], pair_dev
                 )
+            else:
+                arrived(s_recv.at[pl.ds(at, block)], c_ss.at[k], c_rs.at[k])
+                if k:
+                    s_mine[pl.ds(at, block), :] += s_recv[pl.ds(at, block), :]
+                    send(
+                        s_mine.at[pl.ds(at, block)], x_recv.at[k - 1], x_ss.at[k - 1], x_rs.at[k - 1],
+                        device(core, q_to(k), z),
+                    )
+            if gram_steps and n == min(2, len(turns) - 1):
+                gram_steps[0]()
         if gram_steps:
             gram_steps[1]()
         own = q_rows(0)
@@ -359,7 +358,7 @@
             *(one_step * POWER),
         ],
         compiler_params=pltpu.CompilerParams(
-            collective_id=0, has_side_effects=True, vmem_limit_bytes=48 * 1024 * 1024
+            collective_id=0, has_side_effects=True, vmem_limit_bytes=63 * 1024 * 1024
         ),
         name="power_steps",
     )(outcomes, sketch)

time: 75.9 us -> 78 us (1.028)
  Pallas kernels: 70.9 us -> 73.9 us
  local copies, waits for them, and re-layouts: 4.19 us -> 3.24 us
    pallas_call x1, Pallas kernels: 70.9 us -> 73.9 us  [per_device(): pl.pallas_call(functools.partial(power_kernel, sizes, units), out_shape=(...]
    unnamed x6 -> x2, local copies, waits for them, and re-layouts: 4.19 us -> 3.24 us
where the time goes in v3:
time: 78 us; the launch traced here: 77.8 us
  Pallas kernels  73.9 us (95%)
  local copies, waits for them, and re-layouts  3.24 us (4%)
    pallas_call x1, Pallas kernels, per_device(): pl.pallas_call(functools.partial(power_kernel, sizes, units), out_shape=(...  73.9 us
    unnamed x2, local copies, waits for them, and re-layouts  3.24 us

profile of v3, /device:TPU:1, one launch (start us, length us, event | category | flops | bytes accessed | tf_op | source)
XLA Modules:
  0.0 77.8 jit_solution(10885015461379734510)
XLA Ops:
  0.6 73.9 %power_steps.1 = (f32[768,128]{1,0:T(8,128)}, f32[128,128]{1,0:T(8,128)}) custom-call(bf16[768,2048]{1,0:T(8,128)(2,1)} %o_hbm.1, bf16[768,128]{1,0:T(8,128)(2,1)} %c_ref.1), custom_call_target="tpu_custom_call" | custom-call | tf_op jit(solution)/shard_map/power_steps/pallas_call | solution.py:346
  74.5 1.8 %copy.6 = f32[768,128]{1,0:T(8,128)} copy(f32[768,128]{1,0:T(8,128)} %get-tuple-element.4) | data formatting | bytes 786432
  76.3 1.5 %copy.7 = f32[128,128]{1,0:T(8,128)} copy(f32[128,128]{1,0:T(8,128)} %get-tuple-element.5) | data formatting | bytes 131072
